TPU v7x, 128 devices: a whole 4x4x4 slice. The times are simulated.
128 devices in a mesh: ens: 1, feat: 128 (over z, y, x, core).
Axes of the slice: x: 4, y: 4, z: 4, core: 2. Of those that a mesh axis runs over, the one named last changes fastest.
Arguments:
- particles: float32 [2, 256, 32768], P('ens', None, 'feat')
- target_mean: float32 [2, 32768], P('ens', 'feat')
- precision: float32 [32768], P(('ens', 'feat'))
- low_factor: bfloat16 [32768, 64], P(('ens', 'feat'))
Outputs:
- output: float32 [2, 256, 32768], P('ens', None, 'feat')
All inputs are finite; a program needn't handle non-finite values.
Results may differ from a plain program's by a relative error of at most 0.001.
Values are sent between devices in bfloat16 or wider.
A program may use at most 1 GiB of HBM per device.

v0:
```python
import jax
import jax.numpy as jnp
from jax import lax
from jax.sharding import PartitionSpec as P

NUM_STEPS = 3


def solution(mesh):
    feat_count = mesh.shape["feat"]
    data_spec = P("ens", None, "feat")
    mean_spec = P("ens", "feat")
    prec_spec = P(("ens", "feat"))
    factor_spec = P(("ens", "feat"), None)

    def local_steps(particles, target_mean, precision, low_factor):
        num_part = particles.shape[1]
        total_feat = particles.shape[2] * feat_count
        bandwidth = 2.0 * total_feat
        step_size = 0.25 * total_feat
        mean_rows = target_mean[:, None, :]
        theta = particles
        for step_index in range(NUM_STEPS):
            centered = theta - mean_rows
            theta_bf = theta.astype(jnp.bfloat16)
            proj_part = jnp.einsum("end,dr->enr", centered.astype(jnp.bfloat16), low_factor, preferred_element_type=jnp.float32)
            gram_part = jnp.einsum("end,emd->enm", theta_bf, theta_bf, preferred_element_type=jnp.float32)
            project, gram_mat = lax.psum((proj_part, gram_part), "feat")
            gram_diag = jnp.diagonal(gram_mat, axis1=1, axis2=2)
            sq_dist = jnp.maximum(gram_diag[:, :, None] + gram_diag[:, None, :] - 2.0 * gram_mat, 0.0)
            kernel = jnp.exp(-sq_dist / bandwidth)
            low_term = jnp.einsum("enr,dr->end", project.astype(jnp.bfloat16), low_factor, preferred_element_type=jnp.float32)
            grad_log = -(centered * precision + low_term)
            mixed = (grad_log - (2.0 / bandwidth) * theta).astype(jnp.bfloat16)
            drive = jnp.einsum("enm,emd->end", kernel.astype(jnp.bfloat16), mixed, preferred_element_type=jnp.float32)
            row_sum = jnp.sum(kernel, axis=2, keepdims=True)
            theta = theta + step_size * ((drive + (2.0 / bandwidth) * row_sum * theta) / num_part)
        return theta

    return jax.shard_map(local_steps, mesh=mesh, in_specs=(data_spec, mean_spec, prec_spec, factor_spec), out_specs=data_spec, check_vma=False)
```

profile of v0, /device:TPU:1, one launch (start us, length us, event | category | flops | bytes accessed | tf_op | source)
XLA Modules:
  0.0 529.4 jit_solution(13238995211418079603)
XLA Ops:
  6.5 0.0 all-reduce.7.cloned.1.call-start
  6.6 2.3 fusion.67
  8.9 0.0 all-reduce.9.cloned.1.call-start
  9.0 1.2 fusion.33
  10.2 70.4 %all-reduce.12 = bf16[2,256,64]{2,1,0:T(8,128)(2,1)S(1)} all-reduce(f32[2,256,64]{2,1,0:T(8,128)S(1)} %fusion.33), channel_id=1, replica_groups=mesh['ens'=1,'feat'=128] {'feat'}, use_global_device_ids=true, to_apply=%region_1.0 | all-reduce | flops 32768 | bytes 196608 | tf_op jit(solution)/shard_map/psum | solution.py:28
  80.6 83.5 %all-reduce.7.cloned.1.call-done = f32[2,256,256]{2,1,0:T(8,128)} async-done(((f32[2,256,256]{2,1,0:T(8,128)}), f32[2,256,256]{2,1,0:T(8,128)}) %all-reduce.7.cloned.1.call-update) | async-done | bytes 524304 | tf_op jit(solution)/shard_map/psum | solution.py:28
  164.2 17.2 %copy.14 = f32[2,256,256]{0,2,1:T(8,128)} copy(f32[2,256,256]{2,1,0:T(8,128)} %all-reduce.7.cloned.1.call-done) | data formatting | bytes 1048576 | tf_op jit(solution)/shard_map/psum | solution.py:28
  181.4 2.3 gather_fusion
  183.7 0.1 copy.15
  183.8 0.3 fusion.24
  184.2 0.5 fusion.8
  184.7 1.1 fusion.42
  185.7 0.0 all-reduce.9.cloned.1.call-update
  185.8 0.0 all-reduce.11.cloned.1.call-start
  185.8 0.2 fusion.34
  186.0 65.0 %all-reduce.13 = bf16[2,256,64]{2,1,0:T(8,128)(2,1)S(1)} all-reduce(f32[2,256,64]{2,1,0:T(8,128)S(1)} %fusion.34), channel_id=1, replica_groups=mesh['ens'=1,'feat'=128] {'feat'}, use_global_device_ids=true, to_apply=%region_4.5 | all-reduce | flops 32768 | bytes 196608 | tf_op jit(solution)/shard_map/psum | solution.py:28
  251.0 81.8 %all-reduce.9.cloned.1.call-done = f32[2,256,256]{2,1,0:T(8,128)} async-done(((f32[2,256,256]{2,1,0:T(8,128)}), f32[2,256,256]{2,1,0:T(8,128)}) %all-reduce.9.cloned.1.call-update) | async-done | bytes 524304 | tf_op jit(solution)/shard_map/psum | solution.py:28
  332.8 17.2 %copy.17 = f32[2,256,256]{0,2,1:T(8,128)} copy(f32[2,256,256]{2,1,0:T(8,128)} %all-reduce.9.cloned.1.call-done) | data formatting | bytes 1048576 | tf_op jit(solution)/shard_map/psum | solution.py:28
  350.1 2.3 gather_fusion.1
  352.4 0.1 copy.18
  352.5 0.3 fusion.26
  352.8 0.5 fusion.6
  353.3 1.1 fusion.38
  354.4 0.0 all-reduce.11.cloned.1.call-update
  354.4 0.2 fusion.35
  354.6 65.0 %all-reduce.14 = bf16[2,256,64]{2,1,0:T(8,128)(2,1)S(1)} all-reduce(f32[2,256,64]{2,1,0:T(8,128)S(1)} %fusion.35), channel_id=1, replica_groups=mesh['ens'=1,'feat'=128] {'feat'}, use_global_device_ids=true, to_apply=%region_7.8 | all-reduce | flops 32768 | bytes 196608 | tf_op jit(solution)/shard_map/psum | solution.py:28
  419.6 82.0 %all-reduce.11.cloned.1.call-done = f32[2,256,256]{2,1,0:T(8,128)} async-done(((f32[2,256,256]{2,1,0:T(8,128)}), f32[2,256,256]{2,1,0:T(8,128)}) %all-reduce.11.cloned.1.call-update) | async-done | bytes 524304 | tf_op jit(solution)/shard_map/psum | solution.py:28
  501.6 17.2 %copy.20 = f32[2,256,256]{0,2,1:T(8,128)} copy(f32[2,256,256]{2,1,0:T(8,128)} %all-reduce.11.cloned.1.call-done) | data formatting | bytes 1048576 | tf_op jit(solution)/shard_map/psum | solution.py:28
  518.8 2.3 gather_fusion.2
  521.2 0.1 copy.21
  521.2 0.3 fusion.28
  521.5 1.3 fusion.4
  (19 shorter events, 0.1 us)
Async XLA Ops:
  6.5 2.4 copy-start
  6.5 177.6 %copy-start.4 = (f32[2,256,256]{2,1,0:T(8,128)S(1)}, f32[2,256,256]{2,1,0:T(8,128)}, u32[]{:S(2)}) copy-start(f32[2,256,256]{2,1,0:T(8,128)} %param.4) | copy-start | bytes 1572868
  6.5 177.6 %copy-start.5 = (f32[2,256]{1,0:T(2,128)S(1)}, f32[2,256]{1,0:T(2,128)}, u32[]{:S(2)}) copy-start(f32[2,256]{1,0:T(2,128)} %param.5) | copy-start | bytes 6148
  6.5 177.6 %copy-start.6 = (f32[256]{0:T(256)S(1)}, f32[256]{0:T(256)}, u32[]{:S(2)}) copy-start(f32[256]{0:T(256)} %param.6) | copy-start | bytes 3076
  6.5 157.6 %all-reduce.7.cloned.1.call-start = ((), (), s32[]{:S(2)}) async-start(), calls=%async_computation | async-start | bytes 1048576 | tf_op jit(solution)/shard_map/psum | solution.py:28
  8.9 323.9 %all-reduce.9.cloned.1.call-start = ((), (), s32[]{:S(2)}) async-start(), calls=%async_computation.1 | async-start | bytes 1048576 | tf_op jit(solution)/shard_map/psum | solution.py:28
  164.2 19.6 %copy-start.1 = (f32[2,256,256]{2,1,0:T(8,128)S(1)}, f32[2,256,256]{2,1,0:T(8,128)}, u32[]{:S(2)}) copy-start(f32[2,256,256]{2,1,0:T(8,128)} %all-reduce.7.cloned.1.call-done) | copy-start | bytes 1572868
  185.8 315.8 %all-reduce.11.cloned.1.call-start = ((), (), s32[]{:S(2)}) async-start(), calls=%async_computation.2 | async-start | bytes 1048576 | tf_op jit(solution)/shard_map/psum | solution.py:28
  332.8 19.6 %copy-start.2 = (f32[2,256,256]{2,1,0:T(8,128)S(1)}, f32[2,256,256]{2,1,0:T(8,128)}, u32[]{:S(2)}) copy-start(f32[2,256,256]{2,1,0:T(8,128)} %all-reduce.9.cloned.1.call-done) | copy-start | bytes 1572868
  501.6 19.6 %copy-start.3 = (f32[2,256,256]{2,1,0:T(8,128)S(1)}, f32[2,256,256]{2,1,0:T(8,128)}, u32[]{:S(2)}) copy-start(f32[2,256,256]{2,1,0:T(8,128)} %all-reduce.11.cloned.1.call-done) | copy-start | bytes 1572868
Sparse Core Ops, SparseCore 0:
  12.1 152.0 all-reduce.6
  185.9 146.9 all-reduce.8
  354.5 147.0 all-reduce.10
where the time goes:
time: 531 us; the launch traced here: 529 us
  waiting for transfers between devices  247 us (47%)
  blocking collectives  200 us (38%)
  local copies, waits for them, and re-layouts  58.9 us (11%)
  between operations  13.2 us (2%)
  matrix products  8.44 us (2%)
    psum x3, waiting for transfers between devices, local_steps(): project, gram_mat = lax.psum((proj_part, gram_part), 'feat')  247 us
    psum x3, blocking collectives, local_steps(): project, gram_mat = lax.psum((proj_part, gram_part), 'feat')  200 us
    psum x3, local copies, waits for them, and re-layouts, local_steps(): project, gram_mat = lax.psum((proj_part, gram_part), 'feat')  51.7 us
  transfers between devices with their start and end apart: 3, of which 3 were waited for; matrix products, arithmetic and copies ran while one was open for 0% of the time, Pallas kernels for 0%

commit v1 on v0

v1 whole, which is shorter than its diff:
```python
import functools

import jax
import jax.numpy as jnp
from jax import lax
from jax.experimental import pallas as pl
from jax.experimental.pallas import tpu as pltpu
from jax.sharding import PartitionSpec as P

NUM_STEPS = 3
SIDE = 4
CHIPS = SIDE ** 3
HALF = 128
MESH = pl.DeviceIdType.MESH
NT = (((1,), (1,)), ((), ()))


def _hops(offset):
    return sum(min(d, SIDE - d) for d in offset)


OFFSETS = sorted(
    [(a, b, c) for a in range(SIDE) for b in range(SIDE) for c in range(SIDE) if (a, b, c) != (0, 0, 0)],
    key=lambda offset: -_hops(offset),
)


def _kernel(consts, part_ref, mean_ref, prec_ref, factor_ref, out_ref,
            theta, mean_x, prec_x, factor_x, rs_send, rs_recv, gather, u_lo, u_hi,
            load_sem, swap_send, swap_recv, rs_ssem, rs_rsem, ag_ssem, ag_rsem, out_sem, back_send, back_recv):
    two_over_h, inv_h, step_size, inv_part = consts
    feat = factor_ref.shape[0]
    rank = factor_ref.shape[1]
    f32, bf16 = jnp.float32, jnp.bfloat16
    ens = lax.axis_index("ens")
    me = lax.axis_index("feat")
    core = me % 2
    chip = me // 2
    px, py, pz = chip % SIDE, (chip // SIDE) % SIDE, chip // (SIDE * SIDE)
    partner = chip * 2 + (1 - core)

    def peer(offset):
        dz, dy, dx = offset
        tz, ty, tx = (pz + dz) % SIDE, (py + dy) % SIDE, (px + dx) % SIDE
        return (tz * SIDE + ty) * SIDE + tx

    barrier = pltpu.get_barrier_semaphore()
    for offset in OFFSETS:
        pl.semaphore_signal(barrier, inc=1, device_id=(ens, peer(offset) * 2 + core), device_id_type=MESH)
    pl.semaphore_signal(barrier, inc=1, device_id=(ens, partner), device_id_type=MESH)
    load = pltpu.make_async_copy(part_ref.at[core], theta.at[:, pl.ds(0, feat)], load_sem)
    load.start()
    pl.semaphore_wait(barrier, CHIPS)

    swaps = []
    for k, (src, dst) in enumerate((
        (part_ref.at[1 - core], theta.at[:, pl.ds(feat, feat)]),
        (mean_ref, mean_x), (prec_ref, prec_x), (factor_ref, factor_x),
    )):
        copy = pltpu.make_async_remote_copy(src, dst, swap_send.at[k], swap_recv.at[k], device_id=(ens, partner), device_id_type=MESH)
        copy.start()
        swaps.append(copy)
    load.wait()
    for copy in swaps:
        copy.wait_recv()

    row_id = lax.broadcasted_iota(jnp.int32, (HALF, HALF), 0)
    col_id = lax.broadcasted_iota(jnp.int32, (HALF, HALF), 1)
    eye, upper = row_id == col_id, row_id <= col_id

    for part, ref in enumerate((factor_ref, factor_x)):
        rows = pl.ds(part * feat, feat)
        zeros = jnp.zeros((feat, HALF - rank), bf16)
        u_lo[rows, :] = jnp.concatenate([ref[...], zeros], axis=1)
        u_hi[rows, :] = jnp.concatenate([zeros, ref[...]], axis=1)
    mean_row = jnp.concatenate([mean_ref[pl.ds(core, 1), :], mean_x[pl.ds(core, 1), :]], axis=1)
    prec_row = jnp.concatenate([prec_ref[...], prec_x[...]], axis=1)

    def partials():
        th = theta[...]
        tb = th.astype(bf16)
        xb = (th - mean_row).astype(bf16)
        top = lax.dot_general(tb[:HALF], tb, NT, preferred_element_type=f32)
        low = lax.dot_general(tb[HALF:], tb[HALF:], NT, preferred_element_type=f32)
        proj = (jnp.dot(xb[:HALF], u_lo[...], preferred_element_type=f32)
                + jnp.dot(xb[HALF:], u_hi[...], preferred_element_type=f32))
        tri = jnp.where(upper, top[:, :HALF], low)
        cross = top[:, HALF:]
        diag = jnp.sum(jnp.where(eye, low, 0.0), axis=0, keepdims=True)
        for o in range(CHIPS):
            block, r = (cross, 4 * o) if o < CHIPS // 2 else (tri, 4 * o - HALF)
            rs_send[o, 0:4, :] = block[r:r + 4]
            rs_send[o, 4:6, :] = proj[2 * o:2 * o + 2]
            rs_send[o, 6:7, :] = diag

    def all_reduce():
        for offset in OFFSETS:
            target = peer(offset)
            pltpu.make_async_remote_copy(
                rs_send.at[target], rs_recv.at[chip], rs_ssem, rs_rsem,
                device_id=(ens, target * 2 + core), device_id_type=MESH).start()
        rs_recv[chip] = rs_send[chip]
        others = pl.ds(0, CHIPS - 1)
        pltpu.make_async_copy(rs_recv.at[others], rs_recv.at[others], rs_rsem).wait()
        total = rs_recv[0]
        for o in range(1, CHIPS):
            total = total + rs_recv[o]
        gather[chip] = total[:6]
        for offset in OFFSETS:
            target = peer(offset)
            pltpu.make_async_remote_copy(
                gather.at[chip], gather.at[chip], ag_ssem, ag_rsem,
                device_id=(ens, target * 2 + core), device_id_type=MESH).start()
        pltpu.make_async_copy(gather.at[others], gather.at[others], ag_rsem).wait()
        pltpu.make_async_copy(rs_send.at[others], rs_send.at[others], rs_ssem).wait()
        pltpu.make_async_copy(gather.at[others], gather.at[others], ag_ssem).wait()
        return total[6:7]

    def update(diag):
        cross = jnp.concatenate([gather[o, 0:4, :] for o in range(CHIPS // 2)], axis=0)
        tri = jnp.concatenate([gather[o, 0:4, :] for o in range(CHIPS // 2, CHIPS)], axis=0)
        proj = jnp.concatenate([gather[o, 4:6, :] for o in range(CHIPS)], axis=0).astype(bf16)
        tri_t, cross_t = tri.T, cross.T
        g_aa = jnp.where(upper, tri, tri_t)
        g_cc = jnp.where(eye, diag, jnp.where(upper, tri_t, tri))
        row_a = jnp.sum(jnp.where(eye, tri, 0.0), axis=0, keepdims=True)
        col_a = jnp.sum(jnp.where(eye, tri, 0.0), axis=1, keepdims=True)
        col_c = jnp.sum(jnp.where(eye, diag, 0.0), axis=1, keepdims=True)
        top = jnp.concatenate([g_aa, cross], axis=1)
        bottom = jnp.concatenate([cross_t, g_cc], axis=1)
        row_all = jnp.concatenate([row_a, diag], axis=1)
        k_top = jnp.exp(-jnp.maximum(col_a + row_all - 2.0 * top, 0.0) * inv_h)
        k_bot = jnp.exp(-jnp.maximum(col_c + row_all - 2.0 * bottom, 0.0) * inv_h)
        kernel = jnp.concatenate([k_top, k_bot], axis=0)
        row_sum = jnp.sum(kernel, axis=1, keepdims=True)
        kernel_bf = kernel.astype(bf16)
        for part in range(2):
            cols = slice(part * feat, (part + 1) * feat)
            th = theta[:, cols]
            low = jnp.concatenate([
                lax.dot_general(proj, u_lo[cols, :], NT, preferred_element_type=f32),
                lax.dot_general(proj, u_hi[cols, :], NT, preferred_element_type=f32)], axis=0)
            grad = -((th - mean_row[:, cols]) * prec_row[:, cols] + low)
            mixed = (grad - two_over_h * th).astype(bf16)
            drive = jnp.dot(kernel_bf, mixed, preferred_element_type=f32)
            theta[:, cols] = th + step_size * ((drive + two_over_h * row_sum * th) * inv_part)

    partials()

    @pl.loop(0, NUM_STEPS - 1)
    def _(_):
        update(all_reduce())
        partials()

    update(all_reduce())

    back = pltpu.make_async_remote_copy(theta.at[:, pl.ds(feat, feat)], out_ref.at[core], back_send, back_recv, device_id=(ens, partner), device_id_type=MESH)
    back.start()
    keep = pltpu.make_async_copy(theta.at[:, pl.ds(0, feat)], out_ref.at[core], out_sem)
    keep.start()
    for copy in swaps:
        copy.wait_send()
    keep.wait()
    pltpu.make_async_remote_copy(theta.at[:, pl.ds(feat, feat)], out_ref.at[1 - core], back_send, back_recv, device_id=(ens, partner), device_id_type=MESH).wait()


def solution(mesh):
    feat_count = mesh.shape["feat"]
    data_spec = P("ens", None, "feat")
    mean_spec = P("ens", "feat")
    prec_spec = P(("ens", "feat"))
    factor_spec = P(("ens", "feat"), None)

    def local_steps(particles, target_mean, precision, low_factor):
        _, num_part, feat = particles.shape
        rank = low_factor.shape[1]
        total_feat = feat * feat_count
        bandwidth = 2.0 * total_feat
        consts = (2.0 / bandwidth, 1.0 / bandwidth, 0.25 * total_feat, 1.0 / num_part)
        vmem, hbm = pl.BlockSpec(memory_space=pltpu.VMEM), pl.BlockSpec(memory_space=pl.ANY)
        dma = pltpu.SemaphoreType.DMA
        return pl.pallas_call(
            functools.partial(_kernel, consts),
            name="svgd",
            out_shape=jax.ShapeDtypeStruct(particles.shape, jnp.float32),
            in_specs=[hbm, vmem, vmem, vmem],
            out_specs=hbm,
            scratch_shapes=[
                pltpu.VMEM((num_part, 2 * feat), jnp.float32),
                pltpu.VMEM((2, feat), jnp.float32),
                pltpu.VMEM((1, feat), jnp.float32),
                pltpu.VMEM((feat, rank), jnp.bfloat16),
                pltpu.VMEM((CHIPS, 7, HALF), jnp.float32),
                pltpu.VMEM((CHIPS, 7, HALF), jnp.float32),
                pltpu.VMEM((CHIPS, 6, HALF), jnp.float32),
                pltpu.VMEM((2 * feat, HALF), jnp.bfloat16),
                pltpu.VMEM((2 * feat, HALF), jnp.bfloat16),
                dma, dma((4,)), dma((4,)), dma, dma, dma, dma, dma, dma, dma,
            ],
            compiler_params=pltpu.CompilerParams(collective_id=0, has_side_effects=True),
        )(particles, target_mean, precision.reshape(1, feat), low_factor)

    return jax.shard_map(local_steps, mesh=mesh, in_specs=(data_spec, mean_spec, prec_spec, factor_spec), out_specs=data_spec, check_vma=False)
```

time: 531 us -> 57 us (0.11)
  waiting for transfers between devices: 247 us -> 0 us
  blocking collectives: 200 us -> 0 us
  local copies, waits for them, and re-layouts: 58.9 us -> 3.36 us
  Pallas kernels: 0 us -> 53.3 us
  between operations: 13.2 us -> 0.01 us
  matrix products: 8.44 us -> 0 us
    psum x3 -> x0, waiting for transfers between devices: 247 us -> none  [local_steps(): project, gram_mat = lax.psum((proj_part, gram_part), 'feat')]
    psum x3 -> x0, blocking collectives: 200 us -> none  [local_steps(): project, gram_mat = lax.psum((proj_part, gram_part), 'feat')]
    pallas_call x0 -> x1, Pallas kernels: none -> 53.3 us  [local_steps(): pl.pallas_call(functools.partial(_kernel, consts), name='svgd', out_shape...]
    psum x3 -> x0, local copies, waits for them, and re-layouts: 51.7 us -> none  [local_steps(): project, gram_mat = lax.psum((proj_part, gram_part), 'feat')]
    dot_general x9 -> x0, matrix products: 8.44 us -> none  [the longest x3 4.42 us: local_steps(): jnp.einsum('end,emd->enm', theta_bf, theta_bf, preferred_element_type=jnp...]
    gather x6 -> x0, local copies, waits for them, and re-layouts: 7.18 us -> none  [local_steps(): gram_diag = jnp.diagonal(gram_mat, axis1=1, axis2=2)]
  transfers between devices with their start and end apart: 3 -> 0, of which waited for: 3 -> 0; matrix products, arithmetic and copies ran while one was open for 0% -> 0% of each run, Pallas kernels for 0% -> 0%
where the time goes in v1:
time: 57 us; the launch traced here: 56.7 us
  Pallas kernels  53.3 us (94%)
  local copies, waits for them, and re-layouts  3.36 us (6%)
    pallas_call x1, Pallas kernels, local_steps(): pl.pallas_call(functools.partial(_kernel, consts), name='svgd', out_shape...  53.3 us
    unnamed x2, local copies, waits for them, and re-layouts  3.36 us

profile of v1, /device:TPU:1, one launch (start us, length us, event | category | flops | bytes accessed | tf_op | source)
XLA Modules:
  0.0 56.7 jit_solution(10711500782957966565)
XLA Ops:
  0.0 1.5 %copy.5.factor_ref = bf16[256,64]{1,0:T(8,128)(2,1)} copy(bf16[256,64]{0,1:T(8,128)(2,1)} %param.7) | data formatting | bytes 65536 | tf_op args[3]
  1.5 53.3 %svgd.1 = f32[2,256,256]{2,1,0:T(8,128)} custom-call(f32[2,256,256]{2,1,0:T(8,128)} %part_ref.1, f32[2,256]{1,0:T(2,128)} %mean_ref.1, f32[1,256]{1,0:T(1,128)} %bitcast.1, bf16[256,64]{1,0:T(8,128)(2,1)} %copy.5.factor_ref), custom_call_target="tpu_custom_call" | custom-call | tf_op jit(solution)/shard_map/svgd/pallas_call | solution.py:182
  54.8 1.9 %copy.7 = f32[2,256,256]{2,1,0:T(8,128)} copy(f32[2,256,256]{2,1,0:T(8,128)} %svgd.1) | data formatting | bytes 1048576

commit v2 on v1

v2 whole, which is shorter than its diff:
```python
import functools

import jax
import jax.numpy as jnp
from jax import lax
from jax.experimental import pallas as pl
from jax.experimental.pallas import tpu as pltpu
from jax.sharding import PartitionSpec as P

NUM_STEPS = 3
SIDE = 4
CHIPS = SIDE ** 3
HALF = 128
MESH = pl.DeviceIdType.MESH
NT = (((1,), (1,)), ((), ()))


def _hops(offset):
    return sum(min(d, SIDE - d) for d in offset)


OFFSETS = sorted(
    [(a, b, c) for a in range(SIDE) for b in range(SIDE) for c in range(SIDE) if (a, b, c) != (0, 0, 0)],
    key=lambda offset: -_hops(offset),
)


def _kernel(consts, part_ref, mean_ref, prec_ref, factor_ref, out_ref,
            theta, spare, mean_own, mean_x, prec_own, prec_x, factor_own, factor_x, rs_send, rs_recv, gather, u_lo, u_hi,
            load_sem, swap_send, swap_recv, hello, go, rs_ssem, rs_rsem, ag_ssem, ag_rsem, back_send, back_recv):
    two_over_h, inv_h, step_size, inv_part = consts
    rank, feat = factor_ref.shape
    f32, bf16 = jnp.float32, jnp.bfloat16
    ens = lax.axis_index("ens")
    me = lax.axis_index("feat")
    core = me % 2
    chip = me // 2
    px, py, pz = chip % SIDE, (chip // SIDE) % SIDE, chip // (SIDE * SIDE)
    partner = chip * 2 + (1 - core)

    def peer(offset):
        dz, dy, dx = offset
        tz, ty, tx = (pz + dz) % SIDE, (py + dy) % SIDE, (px + dx) % SIDE
        return (tz * SIDE + ty) * SIDE + tx

    barrier = pltpu.get_barrier_semaphore()

    @pl.when(core == 0)
    def _():
        pl.semaphore_signal(barrier, inc=1, device_id=(ens, partner), device_id_type=MESH)

    loads = []
    for k, (src, dst) in enumerate((
        (part_ref.at[1 - core], spare), (part_ref.at[core], theta.at[:, pl.ds(0, feat)]),
        (mean_ref, mean_own), (prec_ref, prec_own), (factor_ref, factor_own),
    )):
        copy = pltpu.make_async_copy(src, dst, load_sem.at[k])
        copy.start()
        loads.append(copy)

    @pl.when(core == 1)
    def _():
        pl.semaphore_wait(barrier, 1)
        pl.semaphore_signal(hello, inc=1, device_id=(ens, partner), device_id_type=MESH)

    @pl.when(core == 0)
    def _():
        pl.semaphore_wait(hello, 1)
        for offset in OFFSETS:
            pl.semaphore_signal(barrier, inc=1, device_id=(ens, peer(offset) * 2), device_id_type=MESH)

    swaps = []
    for k, (load, src, dst) in enumerate((
        (loads[0], spare, theta.at[:, pl.ds(feat, feat)]), (loads[2], mean_own, mean_x),
        (loads[3], prec_own, prec_x), (loads[4], factor_own, factor_x),
    )):
        load.wait()
        copy = pltpu.make_async_remote_copy(src, dst, swap_send.at[k], swap_recv.at[k], device_id=(ens, partner), device_id_type=MESH)
        copy.start()
        swaps.append(copy)
    loads[1].wait()

    row_id = lax.broadcasted_iota(jnp.int32, (HALF, HALF), 0)
    col_id = lax.broadcasted_iota(jnp.int32, (HALF, HALF), 1)
    eye, upper = row_id == col_id, row_id <= col_id

    zeros = jnp.zeros((HALF - rank, 2 * feat), bf16)
    u_lo[rank:, :] = zeros
    u_hi[:HALF - rank, :] = zeros
    for copy in swaps:
        copy.wait_recv()
    factor = jnp.concatenate([factor_own[...], factor_x[...]], axis=1)
    u_lo[:rank, :] = factor
    u_hi[HALF - rank:, :] = factor
    mean_row = jnp.concatenate([mean_own[pl.ds(core, 1), :], mean_x[pl.ds(core, 1), :]], axis=1)
    prec_row = jnp.concatenate([prec_own[...], prec_x[...]], axis=1)
    others = pl.ds(0, CHIPS - 1)

    def drain(ref, sem):
        pltpu.make_async_copy(ref.at[others], ref.at[others], sem).wait()

    def partials():
        th = theta[...]
        tb = th.astype(bf16)
        xb = (th - mean_row).astype(bf16)
        top = lax.dot_general(tb[:HALF], tb, NT, preferred_element_type=f32)
        low = lax.dot_general(tb[HALF:], tb[HALF:], NT, preferred_element_type=f32)
        proj = (lax.dot_general(xb[:HALF], u_lo[...], NT, preferred_element_type=f32)
                + lax.dot_general(xb[HALF:], u_hi[...], NT, preferred_element_type=f32))
        tri = jnp.where(upper, top[:, :HALF], low)
        cross = top[:, HALF:]
        diag = jnp.sum(jnp.where(eye, low, 0.0), axis=0, keepdims=True)
        for o in range(CHIPS):
            block, r = (cross, 4 * o) if o < CHIPS // 2 else (tri, 4 * o - HALF)
            rs_send[o, 0:4, :] = block[r:r + 4]
            rs_send[o, 4:6, :] = proj[2 * o:2 * o + 2]
            rs_send[o, 6:7, :] = diag

    def all_reduce(first):
        for offset in OFFSETS:
            target = peer(offset)
            pltpu.make_async_remote_copy(
                rs_send.at[target], rs_recv.at[chip], rs_ssem, rs_rsem,
                device_id=(ens, target * 2 + core), device_id_type=MESH).start()
        rs_recv[chip] = rs_send[chip]
        if not first:
            drain(gather, ag_ssem)
        drain(rs_recv, rs_rsem)
        sums = [rs_recv[o] for o in range(4)]
        for o in range(4, CHIPS):
            sums[o % 4] = sums[o % 4] + rs_recv[o]
        total = (sums[0] + sums[1]) + (sums[2] + sums[3])
        gather[chip] = total[:6]
        for offset in OFFSETS:
            target = peer(offset)
            pltpu.make_async_remote_copy(
                gather.at[chip], gather.at[chip], ag_ssem, ag_rsem,
                device_id=(ens, target * 2 + core), device_id_type=MESH).start()
        drain(rs_send, rs_ssem)
        drain(gather, ag_rsem)
        return total[6:7]

    def update(diag, last):
        cross = jnp.concatenate([gather[o, 0:4, :] for o in range(CHIPS // 2)], axis=0)
        tri = jnp.concatenate([gather[o, 0:4, :] for o in range(CHIPS // 2, CHIPS)], axis=0)
        proj = jnp.concatenate([gather[o, 4:6, :] for o in range(CHIPS)], axis=0).astype(bf16)
        tri_t, cross_t = tri.T, cross.T
        g_aa = jnp.where(upper, tri, tri_t)
        g_cc = jnp.where(eye, diag, jnp.where(upper, tri_t, tri))
        row_a = jnp.sum(jnp.where(eye, tri, 0.0), axis=0, keepdims=True)
        col_a = jnp.sum(jnp.where(eye, tri, 0.0), axis=1, keepdims=True)
        col_c = jnp.sum(jnp.where(eye, diag, 0.0), axis=1, keepdims=True)
        top = jnp.concatenate([g_aa, cross], axis=1)
        bottom = jnp.concatenate([cross_t, g_cc], axis=1)
        row_all = jnp.concatenate([row_a, diag], axis=1)
        k_top = jnp.exp(-jnp.maximum(col_a + row_all - 2.0 * top, 0.0) * inv_h)
        k_bot = jnp.exp(-jnp.maximum(col_c + row_all - 2.0 * bottom, 0.0) * inv_h)
        kernel = jnp.concatenate([k_top, k_bot], axis=0)
        row_sum = jnp.sum(kernel, axis=1, keepdims=True)
        kernel_bf = kernel.astype(bf16)
        for part in (1, 0):
            cols = slice(part * feat, (part + 1) * feat)
            th = theta[:, cols]
            low = jnp.concatenate([
                jnp.dot(proj, u_lo[:, cols], preferred_element_type=f32),
                jnp.dot(proj, u_hi[:, cols], preferred_element_type=f32)], axis=0)
            grad = -((th - mean_row[:, cols]) * prec_row[:, cols] + low)
            mixed = (grad - two_over_h * th).astype(bf16)
            drive = jnp.dot(kernel_bf, mixed, preferred_element_type=f32)
            new = th + step_size * ((drive + two_over_h * row_sum * th) * inv_part)
            if not last:
                theta[:, cols] = new
            elif part == 1:
                spare[...] = new
                back = pltpu.make_async_remote_copy(
                    spare, out_ref.at[core], back_send, back_recv, device_id=(ens, partner), device_id_type=MESH)
                back.start()
            else:
                out_ref[core] = new

    partials()

    @pl.when(core == 0)
    def _():
        pl.semaphore_wait(barrier, CHIPS - 1)
        pl.semaphore_signal(go, inc=1, device_id=(ens, partner), device_id_type=MESH)

    @pl.when(core == 1)
    def _():
        pl.semaphore_wait(go, 1)

    first_diag = all_reduce(True)
    for copy in swaps:
        copy.wait_send()

    def body(_, diag):
        update(diag, False)
        partials()
        return all_reduce(False)

    update(lax.fori_loop(0, NUM_STEPS - 1, body, first_diag), True)
    drain(gather, ag_ssem)
    pltpu.make_async_remote_copy(
        spare, out_ref.at[1 - core], back_send, back_recv, device_id=(ens, partner), device_id_type=MESH).wait()


def solution(mesh):
    feat_count = mesh.shape["feat"]
    data_spec = P("ens", None, "feat")
    mean_spec = P("ens", "feat")
    prec_spec = P(("ens", "feat"))
    factor_spec = P(("ens", "feat"), None)

    def local_steps(particles, target_mean, precision, low_factor):
        _, num_part, feat = particles.shape
        rank = low_factor.shape[1]
        total_feat = feat * feat_count
        bandwidth = 2.0 * total_feat
        consts = (2.0 / bandwidth, 1.0 / bandwidth, 0.25 * total_feat, 1.0 / num_part)
        hbm, vmem = pl.BlockSpec(memory_space=pl.ANY), pl.BlockSpec(memory_space=pltpu.VMEM)
        dma, regular = pltpu.SemaphoreType.DMA, pltpu.SemaphoreType.REGULAR
        f32, bf16 = jnp.float32, jnp.bfloat16
        return pl.pallas_call(
            functools.partial(_kernel, consts),
            name="svgd",
            out_shape=pltpu.VMEM(particles.shape, f32),
            in_specs=[hbm, hbm, hbm, hbm],
            out_specs=vmem,
            scratch_shapes=[
                pltpu.VMEM((num_part, 2 * feat), f32),
                pltpu.VMEM((num_part, feat), f32),
                pltpu.VMEM((2, feat), f32),
                pltpu.VMEM((2, feat), f32),
                pltpu.VMEM((1, feat), f32),
                pltpu.VMEM((1, feat), f32),
                pltpu.VMEM((rank, feat), bf16),
                pltpu.VMEM((rank, feat), bf16),
                pltpu.VMEM((CHIPS, 7, HALF), f32),
                pltpu.VMEM((CHIPS, 7, HALF), f32),
                pltpu.VMEM((CHIPS, 6, HALF), f32),
                pltpu.VMEM((HALF, 2 * feat), bf16),
                pltpu.VMEM((HALF, 2 * feat), bf16),
                dma((5,)), dma((4,)), dma((4,)), regular, regular, dma, dma, dma, dma, dma, dma,
            ],
            compiler_params=pltpu.CompilerParams(collective_id=0, has_side_effects=True),
        )(particles, target_mean, precision.reshape(1, feat), low_factor.T)

    return jax.shard_map(local_steps, mesh=mesh, in_specs=(data_spec, mean_spec, prec_spec, factor_spec), out_specs=data_spec, check_vma=False)
```

time: 57 us -> 52.9 us (0.928)
  local copies, waits for them, and re-layouts: 3.36 us -> 0.8 us
  Pallas kernels: 53.3 us -> 52 us
    unnamed x2 -> x1, local copies, waits for them, and re-layouts: 3.36 us -> 0.8 us
    pallas_call x1, Pallas kernels: 53.3 us -> 52 us  [local_steps(): pl.pallas_call(functools.partial(_kernel, consts), name='svgd', out_shape...]
where the time goes in v2:
time: 52.9 us; the launch traced here: 52.8 us
  Pallas kernels  52 us (98%)
  local copies, waits for them, and re-layouts  0.8 us (2%)
    pallas_call x1, Pallas kernels, local_steps(): pl.pallas_call(functools.partial(_kernel, consts), name='svgd', out_shape...  52 us

profile of v2, /device:TPU:1, one launch (start us, length us, event | category | flops | bytes accessed | tf_op | source)
XLA Modules:
  0.0 52.8 jit_solution(67370986077622840)
XLA Ops:
  0.0 52.0 %svgd.1 = f32[2,256,256]{2,1,0:T(8,128)S(1)} custom-call(f32[2,256,256]{2,1,0:T(8,128)} %part_ref.1, f32[2,256]{1,0:T(2,128)} %mean_ref.1, f32[1,256]{1,0:T(1,128)} %bitcast.3, bf16[64,256]{1,0:T(8,128)(2,1)} %bitcast.2), custom_call_target="tpu_custom_call" | custom-call | tf_op jit(solution)/shard_map/svgd/pallas_call | solution.py:223
  52.0 0.8 %copy.6 = f32[2,256,256]{2,1,0:T(8,128)} copy(f32[2,256,256]{2,1,0:T(8,128)S(1)} %svgd.1) | data formatting | bytes 1048576

commit v3 on v2

--- a/solution.py
+++ b/solution.py
@@ -15,18 +15,15 @@
 NT = (((1,), (1,)), ((), ()))
 
 
-def _hops(offset):
-    return sum(min(d, SIDE - d) for d in offset)
-
-
+COST = (0, 7, 10, 7)
 OFFSETS = sorted(
-    [(a, b, c) for a in range(SIDE) for b in range(SIDE) for c in range(SIDE) if (a, b, c) != (0, 0, 0)],
-    key=lambda offset: -_hops(offset),
+    [(a, b, c) for a in range(SIDE) for b in range(SIDE) for c in range(SIDE)],
+    key=lambda offset: -sum(COST[d] for d in offset),
 )
 
 
 def _kernel(consts, part_ref, mean_ref, prec_ref, factor_ref, out_ref,
-            theta, spare, mean_own, mean_x, prec_own, prec_x, factor_own, factor_x, rs_send, rs_recv, gather, u_lo, u_hi,
+            theta, spare, mean_own, mean_x, prec_own, prec_x, factor_own, factor_x, rs_send, rs_recv, total, gather, u_lo, u_hi,
             load_sem, swap_send, swap_recv, hello, go, rs_ssem, rs_rsem, ag_ssem, ag_rsem, back_send, back_recv):
     two_over_h, inv_h, step_size, inv_part = consts
     rank, feat = factor_ref.shape
@@ -45,7 +42,7 @@
 
     barrier = pltpu.get_barrier_semaphore()
 
-    @pl.when(core == 0)
+    @pl.when(core == 1)
     def _():
         pl.semaphore_signal(barrier, inc=1, device_id=(ens, partner), device_id_type=MESH)
 
@@ -58,16 +55,16 @@
         copy.start()
         loads.append(copy)
 
-    @pl.when(core == 1)
+    @pl.when(core == 0)
     def _():
         pl.semaphore_wait(barrier, 1)
         pl.semaphore_signal(hello, inc=1, device_id=(ens, partner), device_id_type=MESH)
 
-    @pl.when(core == 0)
+    @pl.when(core == 1)
     def _():
         pl.semaphore_wait(hello, 1)
-        for offset in OFFSETS:
-            pl.semaphore_signal(barrier, inc=1, device_id=(ens, peer(offset) * 2), device_id_type=MESH)
+        for offset in OFFSETS[:-1]:
+            pl.semaphore_signal(barrier, inc=1, device_id=(ens, peer(offset) * 2 + 1), device_id_type=MESH)
 
     swaps = []
     for k, (load, src, dst) in enumerate((
@@ -94,10 +91,9 @@
     u_hi[HALF - rank:, :] = factor
     mean_row = jnp.concatenate([mean_own[pl.ds(core, 1), :], mean_x[pl.ds(core, 1), :]], axis=1)
     prec_row = jnp.concatenate([prec_own[...], prec_x[...]], axis=1)
-    others = pl.ds(0, CHIPS - 1)
 
     def drain(ref, sem):
-        pltpu.make_async_copy(ref.at[others], ref.at[others], sem).wait()
+        pltpu.make_async_copy(ref, ref, sem).wait()
 
     def partials():
         th = theta[...]
@@ -121,29 +117,27 @@
             target = peer(offset)
             pltpu.make_async_remote_copy(
                 rs_send.at[target], rs_recv.at[chip], rs_ssem, rs_rsem,
-                device_id=(ens, target * 2 + core), device_id_type=MESH).start()
-        rs_recv[chip] = rs_send[chip]
+                device_id=(ens, target * 2 + (1 - core)), device_id_type=MESH).start()
         if not first:
             drain(gather, ag_ssem)
         drain(rs_recv, rs_rsem)
         sums = [rs_recv[o] for o in range(4)]
         for o in range(4, CHIPS):
             sums[o % 4] = sums[o % 4] + rs_recv[o]
-        total = (sums[0] + sums[1]) + (sums[2] + sums[3])
-        gather[chip] = total[:6]
+        total[...] = (sums[0] + sums[1]) + (sums[2] + sums[3])
         for offset in OFFSETS:
             target = peer(offset)
             pltpu.make_async_remote_copy(
-                gather.at[chip], gather.at[chip], ag_ssem, ag_rsem,
-                device_id=(ens, target * 2 + core), device_id_type=MESH).start()
+                total, gather.at[chip], ag_ssem, ag_rsem,
+                device_id=(ens, target * 2 + (1 - core)), device_id_type=MESH).start()
         drain(rs_send, rs_ssem)
         drain(gather, ag_rsem)
-        return total[6:7]
-
-    def update(diag, last):
+
+    def update(last):
         cross = jnp.concatenate([gather[o, 0:4, :] for o in range(CHIPS // 2)], axis=0)
         tri = jnp.concatenate([gather[o, 0:4, :] for o in range(CHIPS // 2, CHIPS)], axis=0)
         proj = jnp.concatenate([gather[o, 4:6, :] for o in range(CHIPS)], axis=0).astype(bf16)
+        diag = gather[0, 6:7, :]
         tri_t, cross_t = tri.T, cross.T
         g_aa = jnp.where(upper, tri, tri_t)
         g_cc = jnp.where(eye, diag, jnp.where(upper, tri_t, tri))
@@ -180,25 +174,26 @@
 
     partials()
 
-    @pl.when(core == 0)
+    @pl.when(core == 1)
     def _():
         pl.semaphore_wait(barrier, CHIPS - 1)
         pl.semaphore_signal(go, inc=1, device_id=(ens, partner), device_id_type=MESH)
 
-    @pl.when(core == 1)
+    @pl.when(core == 0)
     def _():
         pl.semaphore_wait(go, 1)
 
-    first_diag = all_reduce(True)
+    all_reduce(True)
     for copy in swaps:
         copy.wait_send()
 
-    def body(_, diag):
-        update(diag, False)
+    @pl.loop(0, NUM_STEPS - 1)
+    def _(_):
+        update(False)
         partials()
-        return all_reduce(False)
-
-    update(lax.fori_loop(0, NUM_STEPS - 1, body, first_diag), True)
+        all_reduce(False)
+
+    update(True)
     drain(gather, ag_ssem)
     pltpu.make_async_remote_copy(
         spare, out_ref.at[1 - core], back_send, back_recv, device_id=(ens, partner), device_id_type=MESH).wait()
@@ -237,7 +232,8 @@
                 pltpu.VMEM((rank, feat), bf16),
                 pltpu.VMEM((CHIPS, 7, HALF), f32),
                 pltpu.VMEM((CHIPS, 7, HALF), f32),
-                pltpu.VMEM((CHIPS, 6, HALF), f32),
+                pltpu.VMEM((7, HALF), f32),
+                pltpu.VMEM((CHIPS, 7, HALF), f32),
                 pltpu.VMEM((HALF, 2 * feat), bf16),
                 pltpu.VMEM((HALF, 2 * feat), bf16),
                 dma((5,)), dma((4,)), dma((4,)), regular, regular, dma, dma, dma, dma, dma, dma,

time: 52.9 us -> 50.9 us (0.962)
  Pallas kernels: 52 us -> 50 us
    pallas_call x1, Pallas kernels: 52 us -> 50 us  [local_steps(): pl.pallas_call(functools.partial(_kernel, consts), name='svgd', out_shape...]
where the time goes in v3:
time: 50.9 us; the launch traced here: 50.8 us
  Pallas kernels  50 us (98%)
  local copies, waits for them, and re-layouts  0.8 us (2%)
    pallas_call x1, Pallas kernels, local_steps(): pl.pallas_call(functools.partial(_kernel, consts), name='svgd', out_shape...  50 us

profile of v3, /device:TPU:1, one launch (start us, length us, event | category | flops | bytes accessed | tf_op | source)
XLA Modules:
  0.0 50.8 jit_solution(13732786951574789566)
XLA Ops:
  0.0 50.0 %svgd.1 = f32[2,256,256]{2,1,0:T(8,128)S(1)} custom-call(f32[2,256,256]{2,1,0:T(8,128)} %part_ref.1, f32[2,256]{1,0:T(2,128)} %mean_ref.1, f32[1,256]{1,0:T(1,128)} %bitcast.3, bf16[64,256]{1,0:T(8,128)(2,1)} %bitcast.2), custom_call_target="tpu_custom_call" | custom-call | tf_op jit(solution)/shard_map/svgd/pallas_call | solution.py:218
  50.0 0.8 %copy.6 = f32[2,256,256]{2,1,0:T(8,128)} copy(f32[2,256,256]{2,1,0:T(8,128)S(1)} %svgd.1) | data formatting | bytes 1048576

commit v4 on v3

--- a/solution.py
+++ b/solution.py
@@ -11,6 +11,7 @@
 SIDE = 4
 CHIPS = SIDE ** 3
 HALF = 128
+DIAG_CHIP = 21
 MESH = pl.DeviceIdType.MESH
 NT = (((1,), (1,)), ((), ()))
 
@@ -23,8 +24,8 @@
 
 
 def _kernel(consts, part_ref, mean_ref, prec_ref, factor_ref, out_ref,
-            theta, spare, mean_own, mean_x, prec_own, prec_x, factor_own, factor_x, rs_send, rs_recv, total, gather, u_lo, u_hi,
-            load_sem, swap_send, swap_recv, hello, go, rs_ssem, rs_rsem, ag_ssem, ag_rsem, back_send, back_recv):
+            theta, spare, mean_own, mean_x, prec_own, prec_x, factor_own, factor_x, rs_send, rs_recv, total, gather, diag_send, diag_recv, diag_total, diag_all, u_lo, u_hi,
+            load_sem, swap_send, swap_recv, hello, go, rs_ssem, rs_rsem, ag_ssem, ag_rsem, dr_ssem, dr_rsem, dg_ssem, dg_rsem, back_send, back_recv):
     two_over_h, inv_h, step_size, inv_part = consts
     rank, feat = factor_ref.shape
     f32, bf16 = jnp.float32, jnp.bfloat16
@@ -110,14 +111,17 @@
             block, r = (cross, 4 * o) if o < CHIPS // 2 else (tri, 4 * o - HALF)
             rs_send[o, 0:4, :] = block[r:r + 4]
             rs_send[o, 4:6, :] = proj[2 * o:2 * o + 2]
-            rs_send[o, 6:7, :] = diag
+        diag_send[...] = diag
+
+    def to_chip(src, dst, ssem, rsem, target):
+        return pltpu.make_async_remote_copy(src, dst, ssem, rsem, device_id=(ens, target * 2 + (1 - core)), device_id_type=MESH)
 
     def all_reduce(first):
+        diag_copy = to_chip(diag_send, diag_recv.at[chip], dr_ssem, dr_rsem, DIAG_CHIP)
+        diag_copy.start()
         for offset in OFFSETS:
             target = peer(offset)
-            pltpu.make_async_remote_copy(
-                rs_send.at[target], rs_recv.at[chip], rs_ssem, rs_rsem,
-                device_id=(ens, target * 2 + (1 - core)), device_id_type=MESH).start()
+            to_chip(rs_send.at[target], rs_recv.at[chip], rs_ssem, rs_rsem, target).start()
         if not first:
             drain(gather, ag_ssem)
         drain(rs_recv, rs_rsem)
@@ -125,19 +129,38 @@
         for o in range(4, CHIPS):
             sums[o % 4] = sums[o % 4] + rs_recv[o]
         total[...] = (sums[0] + sums[1]) + (sums[2] + sums[3])
-        for offset in OFFSETS:
-            target = peer(offset)
-            pltpu.make_async_remote_copy(
-                total, gather.at[chip], ag_ssem, ag_rsem,
-                device_id=(ens, target * 2 + (1 - core)), device_id_type=MESH).start()
+
+        @pl.when(chip == DIAG_CHIP)
+        def _():
+            drain(diag_recv, dr_rsem)
+            diag = diag_recv[0]
+            for o in range(1, CHIPS):
+                diag = diag + diag_recv[o]
+            diag_total[...] = diag
+            for offset in OFFSETS:
+                target = peer(offset)
+                to_chip(diag_total, diag_all, dg_ssem, dg_rsem, target).start()
+                to_chip(total, gather.at[chip], ag_ssem, ag_rsem, target).start()
+
+        @pl.when(chip != DIAG_CHIP)
+        def _():
+            for offset in OFFSETS:
+                to_chip(total, gather.at[chip], ag_ssem, ag_rsem, peer(offset)).start()
+
         drain(rs_send, rs_ssem)
+        diag_copy.wait_send()
+        drain(diag_all, dg_rsem)
         drain(gather, ag_rsem)
+
+        @pl.when(chip == DIAG_CHIP)
+        def _():
+            drain(diag_recv, dg_ssem)
 
     def update(last):
         cross = jnp.concatenate([gather[o, 0:4, :] for o in range(CHIPS // 2)], axis=0)
         tri = jnp.concatenate([gather[o, 0:4, :] for o in range(CHIPS // 2, CHIPS)], axis=0)
         proj = jnp.concatenate([gather[o, 4:6, :] for o in range(CHIPS)], axis=0).astype(bf16)
-        diag = gather[0, 6:7, :]
+        diag = diag_all[...]
         tri_t, cross_t = tri.T, cross.T
         g_aa = jnp.where(upper, tri, tri_t)
         g_cc = jnp.where(eye, diag, jnp.where(upper, tri_t, tri))
@@ -230,13 +253,17 @@
                 pltpu.VMEM((1, feat), f32),
                 pltpu.VMEM((rank, feat), bf16),
                 pltpu.VMEM((rank, feat), bf16),
-                pltpu.VMEM((CHIPS, 7, HALF), f32),
-                pltpu.VMEM((CHIPS, 7, HALF), f32),
-                pltpu.VMEM((7, HALF), f32),
-                pltpu.VMEM((CHIPS, 7, HALF), f32),
+                pltpu.VMEM((CHIPS, 6, HALF), f32),
+                pltpu.VMEM((CHIPS, 6, HALF), f32),
+                pltpu.VMEM((6, HALF), f32),
+                pltpu.VMEM((CHIPS, 6, HALF), f32),
+                pltpu.VMEM((1, HALF), f32),
+                pltpu.VMEM((CHIPS, 1, HALF), f32),
+                pltpu.VMEM((1, HALF), f32),
+                pltpu.VMEM((1, HALF), f32),
                 pltpu.VMEM((HALF, 2 * feat), bf16),
                 pltpu.VMEM((HALF, 2 * feat), bf16),
-                dma((5,)), dma((4,)), dma((4,)), regular, regular, dma, dma, dma, dma, dma, dma,
+                dma((5,)), dma((4,)), dma((4,)), regular, regular, dma, dma, dma, dma, dma, dma, dma, dma, dma, dma,
             ],
             compiler_params=pltpu.CompilerParams(collective_id=0, has_side_effects=True),
         )(particles, target_mean, precision.reshape(1, feat), low_factor.T)

time: 50.9 us -> 49.5 us (0.972)
  Pallas kernels: 50 us -> 48.6 us
    pallas_call x1, Pallas kernels: 50 us -> 48.6 us  [local_steps(): pl.pallas_call(functools.partial(_kernel, consts), name='svgd', out_shape...]
where the time goes in v4:
time: 49.5 us; the launch traced here: 49.4 us
  Pallas kernels  48.6 us (98%)
  local copies, waits for them, and re-layouts  0.8 us (2%)
    pallas_call x1, Pallas kernels, local_steps(): pl.pallas_call(functools.partial(_kernel, consts), name='svgd', out_shape...  48.6 us

profile of v4, /device:TPU:1, one launch (start us, length us, event | category | flops | bytes accessed | tf_op | source)
XLA Modules:
  0.0 49.4 jit_solution(4173933071663262442)
XLA Ops:
  0.0 48.6 %svgd.1 = f32[2,256,256]{2,1,0:T(8,128)S(1)} custom-call(f32[2,256,256]{2,1,0:T(8,128)} %part_ref.1, f32[2,256]{1,0:T(2,128)} %mean_ref.1, f32[1,256]{1,0:T(1,128)} %bitcast.3, bf16[64,256]{1,0:T(8,128)(2,1)} %bitcast.2), custom_call_target="tpu_custom_call" | custom-call | tf_op jit(solution)/shard_map/svgd/pallas_call | solution.py:241
  48.6 0.8 %copy.6 = f32[2,256,256]{2,1,0:T(8,128)} copy(f32[2,256,256]{2,1,0:T(8,128)S(1)} %svgd.1) | data formatting | bytes 1048576

commit v5 on v4

v5 whole, which is shorter than its diff:
```python
import functools

import jax
import jax.numpy as jnp
from jax import lax
from jax.experimental import pallas as pl
from jax.experimental.pallas import tpu as pltpu
from jax.sharding import PartitionSpec as P

NUM_STEPS = 3
SIDE = 4
CHIPS = SIDE ** 3
HALF = 128
DIAG_CHIP = 21
EARLY = (0,)
MESH = pl.DeviceIdType.MESH
NT = (((1,), (1,)), ((), ()))


COST = (0, 7, 10, 7)
OFFSETS = sorted(
    [(a, b, c) for a in range(SIDE) for b in range(SIDE) for c in range(SIDE)],
    key=lambda offset: -sum(COST[d] for d in offset),
)


def _kernel(consts, part_ref, mean_ref, prec_ref, factor_ref, out_ref,
            theta, base, spare, mean_own, mean_x, prec_own, prec_x, factor_own, factor_x, rs_send, rs_recv, total, gather, diag_send, diag_recv, diag_total, diag_all, u_lo, u_hi,
            load_sem, swap_send, swap_recv, hello, go, rs_ssem, rs_rsem, ag_ssem, ag_rsem, dr_ssem, dr_rsem, dg_ssem, dg_rsem, ax_ssem, back_send, back_recv):
    two_over_h, inv_h, scale = consts
    rank, feat = factor_ref.shape
    f32, bf16 = jnp.float32, jnp.bfloat16
    ens = lax.axis_index("ens")
    me = lax.axis_index("feat")
    core = me % 2
    chip = me // 2
    px, py, pz = chip % SIDE, (chip // SIDE) % SIDE, chip // (SIDE * SIDE)
    partner = chip * 2 + (1 - core)

    def peer(offset):
        dz, dy, dx = offset
        tz, ty, tx = (pz + dz) % SIDE, (py + dy) % SIDE, (px + dx) % SIDE
        return (tz * SIDE + ty) * SIDE + tx

    barrier = pltpu.get_barrier_semaphore()

    loads = []
    for k, (src, dst) in enumerate((
        (part_ref.at[1 - core], spare), (part_ref.at[core], theta.at[:, pl.ds(0, feat)]),
        (mean_ref, mean_own), (prec_ref, prec_own), (factor_ref, factor_own),
    )):
        copy = pltpu.make_async_copy(src, dst, load_sem.at[k])
        copy.start()
        loads.append(copy)

    @pl.when(core == 1)
    def _():
        pl.semaphore_signal(barrier, inc=1, device_id=(ens, partner), device_id_type=MESH)
        for offset in OFFSETS[:-1]:
            pl.semaphore_signal(barrier, inc=1, device_id=(ens, peer(offset) * 2 + 1), device_id_type=MESH)
        pl.semaphore_wait(hello, 1)

    @pl.when(core == 0)
    def _():
        for offset in OFFSETS:
            pl.semaphore_signal(barrier, inc=1, device_id=(ens, peer(offset) * 2 + 1), device_id_type=MESH)
        pl.semaphore_wait(barrier, 1)
        pl.semaphore_signal(hello, inc=1, device_id=(ens, partner), device_id_type=MESH)

    swaps = []
    for k, (load, src, dst) in enumerate((
        (loads[0], spare, theta.at[:, pl.ds(feat, feat)]), (loads[2], mean_own, mean_x),
        (loads[3], prec_own, prec_x), (loads[4], factor_own, factor_x),
    )):
        load.wait()
        copy = pltpu.make_async_remote_copy(src, dst, swap_send.at[k], swap_recv.at[k], device_id=(ens, partner), device_id_type=MESH)
        copy.start()
        swaps.append(copy)
    loads[1].wait()

    row_id = lax.broadcasted_iota(jnp.int32, (HALF, HALF), 0)
    col_id = lax.broadcasted_iota(jnp.int32, (HALF, HALF), 1)
    eye, upper = row_id == col_id, row_id <= col_id

    zeros = jnp.zeros((HALF - rank, 2 * feat), bf16)
    u_lo[rank:, :] = zeros
    u_hi[:HALF - rank, :] = zeros
    for copy in swaps:
        copy.wait_recv()
    factor = jnp.concatenate([factor_own[...], factor_x[...]], axis=1)
    u_lo[:rank, :] = factor
    u_hi[HALF - rank:, :] = factor
    mean_row = jnp.concatenate([mean_own[pl.ds(core, 1), :], mean_x[pl.ds(core, 1), :]], axis=1)
    prec_row = jnp.concatenate([prec_own[...], prec_x[...]], axis=1)
    others = pl.ds(0, CHIPS - 1)

    def drain(ref, sem):
        pltpu.make_async_copy(ref, ref, sem).wait()

    def partials():
        th = theta[...]
        tb = th.astype(bf16)
        xb = (th - mean_row).astype(bf16)
        top = lax.dot_general(tb[:HALF], tb, NT, preferred_element_type=f32)
        low = lax.dot_general(tb[HALF:], tb[HALF:], NT, preferred_element_type=f32)
        proj = (lax.dot_general(xb[:HALF], u_lo[...], NT, preferred_element_type=f32)
                + lax.dot_general(xb[HALF:], u_hi[...], NT, preferred_element_type=f32))
        tri = jnp.where(upper, top[:, :HALF], low)
        cross = top[:, HALF:]
        diag = jnp.sum(jnp.where(eye, low, 0.0), axis=0, keepdims=True)
        for o in range(CHIPS):
            block, r = (cross, 4 * o) if o < CHIPS // 2 else (tri, 4 * o - HALF)
            rs_send[o, 0:4, :] = block[r:r + 4]
            rs_send[o, 4:6, :] = proj[2 * o:2 * o + 2]
        diag_send[...] = diag

    def to_core(src, dst, ssem, rsem, target, on):
        return pltpu.make_async_remote_copy(src, dst, ssem, rsem, device_id=(ens, target * 2 + on), device_id_type=MESH)

    other = 1 - core

    def scatter():
        to_core(diag_send, diag_recv.at[chip], dr_ssem, dr_rsem, DIAG_CHIP, other).start()
        for offset in OFFSETS:
            target = peer(offset)
            to_core(rs_send.at[target], rs_recv.at[chip], rs_ssem, rs_rsem, target, other).start()

    def reduce():
        drain(rs_recv, rs_rsem)
        sums = [rs_recv[o] for o in range(4)]
        for o in range(4, CHIPS):
            sums[o % 4] = sums[o % 4] + rs_recv[o]
        total[...] = (sums[0] + sums[1]) + (sums[2] + sums[3])

    def reduce_diag():
        drain(diag_recv, dr_rsem)
        sums = [diag_recv[o] for o in range(4)]
        for o in range(4, CHIPS):
            sums[o % 4] = sums[o % 4] + diag_recv[o]
        diag_total[...] = (sums[0] + sums[1]) + (sums[2] + sums[3])

    def all_gather(last):
        @pl.when(chip == DIAG_CHIP)
        def _():
            reduce_diag()
            if last:
                for target in EARLY:
                    to_core(diag_total, diag_all.at[1], dg_ssem, dg_rsem.at[1], target, core).start()
            for offset in OFFSETS:
                to_core(diag_total, diag_all.at[0], dg_ssem, dg_rsem.at[0], peer(offset), other).start()

        if last:
            for target in EARLY:
                @pl.when(chip != target)
                def _():
                    to_core(total, gather.at[1, chip], ax_ssem, ag_rsem.at[1], target, core).start()
        for offset in OFFSETS:
            to_core(total, gather.at[0, chip], ag_ssem, ag_rsem.at[0], peer(offset), other).start()
        drain(rs_send, rs_ssem)
        drain(diag_send, dr_ssem)

    def sent(last):
        drain(gather.at[0], ag_ssem)

        @pl.when(chip == DIAG_CHIP)
        def _():
            drain(diag_recv, dg_ssem)
            if last:
                drain(diag_recv.at[pl.ds(0, len(EARLY))], dg_ssem)

        if last:
            drain(gather.at[1, pl.ds(0, len(EARLY) - 1)], ax_ssem) if len(EARLY) > 1 else None

            @pl.when(jnp.logical_not(early))
            def _():
                drain(total, ax_ssem)

    def kernel_matrix(k):
        diag = diag_all[k]
        cross = jnp.concatenate([gather[k, o, 0:4, :] for o in range(CHIPS // 2)], axis=0)
        tri = jnp.concatenate([gather[k, o, 0:4, :] for o in range(CHIPS // 2, CHIPS)], axis=0)
        proj = jnp.concatenate([gather[k, o, 4:6, :] for o in range(CHIPS)], axis=0).astype(bf16)
        tri_t, cross_t = tri.T, cross.T
        g_aa = jnp.where(upper, tri, tri_t)
        g_cc = jnp.where(eye, diag, jnp.where(upper, tri_t, tri))
        row_a = jnp.sum(jnp.where(eye, tri, 0.0), axis=0, keepdims=True)
        col_a = jnp.sum(jnp.where(eye, tri, 0.0), axis=1, keepdims=True)
        col_c = jnp.sum(jnp.where(eye, diag, 0.0), axis=1, keepdims=True)
        top = jnp.concatenate([g_aa, cross], axis=1)
        bottom = jnp.concatenate([cross_t, g_cc], axis=1)
        row_all = jnp.concatenate([row_a, diag], axis=1)
        k_top = jnp.exp(-jnp.maximum(col_a + row_all - 2.0 * top, 0.0) * inv_h)
        k_bot = jnp.exp(-jnp.maximum(col_c + row_all - 2.0 * bottom, 0.0) * inv_h)
        kernel = jnp.concatenate([k_top, k_bot], axis=0)
        keep = 1.0 + (scale * two_over_h) * jnp.sum(kernel, axis=1, keepdims=True)
        return kernel.astype(bf16), keep, proj

    def moved(kernel_bf, keep, proj, th, still, cols):
        low = jnp.concatenate([
            jnp.dot(proj, u_lo[:, cols], preferred_element_type=f32),
            jnp.dot(proj, u_hi[:, cols], preferred_element_type=f32)], axis=0)
        drive = jnp.dot(kernel_bf, (still - low).astype(bf16), preferred_element_type=f32)
        return keep * th + scale * drive

    own = slice(0, feat)
    early = functools.reduce(jnp.logical_or, [chip == target for target in EARLY])
    partials()
    for copy in swaps:
        copy.wait_send()

    @pl.when(core == 1)
    def _():
        pl.semaphore_wait(barrier, 2 * CHIPS - 1)
        pl.semaphore_signal(go, inc=1, device_id=(ens, partner), device_id_type=MESH)

    @pl.when(core == 0)
    def _():
        pl.semaphore_wait(go, 1)

    @pl.loop(0, NUM_STEPS - 1)
    def _(_):
        scatter()
        base[...] = -((theta[...] - mean_row) * prec_row) - two_over_h * theta[...]
        reduce()
        all_gather(False)
        drain(diag_all.at[0], dg_rsem.at[0])
        drain(gather.at[0], ag_rsem.at[0])
        weights = kernel_matrix(0)
        for part in range(2):
            cols = slice(part * feat, (part + 1) * feat)
            theta[:, cols] = moved(*weights, theta[:, cols], base[:, cols], cols)
        partials()
        sent(False)

    def still(th, mean, prec):
        return -((th - mean) * prec) - two_over_h * th

    scatter()

    def back_copy(src, dst):
        return pltpu.make_async_remote_copy(src, dst, back_send, back_recv, device_id=(ens, partner), device_id_type=MESH)

    @pl.when(early)
    def _():
        back = back_copy(theta.at[:, pl.ds(feat, feat)], spare)
        back.start()
        base[:, own] = still(theta[:, own], mean_own[pl.ds(core, 1), :], prec_own[...])
        back.wait()
        base[:, feat:] = still(spare[...], mean_own[pl.ds(other, 1), :], prec_own[...])

    @pl.when(jnp.logical_not(early))
    def _():
        base[...] = still(theta[...], mean_row, prec_row)

    reduce()
    all_gather(True)
    drain(diag_all.at[0], dg_rsem.at[0])
    drain(gather.at[0], ag_rsem.at[0])

    @pl.when(early)
    def _():
        out_ref[core] = moved(*kernel_matrix(0), theta[:, own], base[:, own], own)
        gather[1, chip] = total[...]
        drain(diag_all.at[1], dg_rsem.at[1])
        drain(gather.at[1, others], ag_rsem.at[1])
        out_ref[other] = moved(*kernel_matrix(1), spare[...], base[:, feat:], own)

    @pl.when(jnp.logical_not(early))
    def _():
        weights = kernel_matrix(0)
        spare[...] = moved(*weights, theta[:, feat:], base[:, feat:], slice(feat, 2 * feat))
        back_copy(spare, out_ref.at[core]).start()
        out_ref[core] = moved(*weights, theta[:, own], base[:, own], own)
        back_copy(spare, out_ref.at[other]).wait()

    sent(True)


def solution(mesh):
    feat_count = mesh.shape["feat"]
    data_spec = P("ens", None, "feat")
    mean_spec = P("ens", "feat")
    prec_spec = P(("ens", "feat"))
    factor_spec = P(("ens", "feat"), None)

    def local_steps(particles, target_mean, precision, low_factor):
        _, num_part, feat = particles.shape
        rank = low_factor.shape[1]
        total_feat = feat * feat_count
        bandwidth = 2.0 * total_feat
        consts = (2.0 / bandwidth, 1.0 / bandwidth, 0.25 * total_feat / num_part)
        hbm, vmem = pl.BlockSpec(memory_space=pl.ANY), pl.BlockSpec(memory_space=pltpu.VMEM)
        dma, regular = pltpu.SemaphoreType.DMA, pltpu.SemaphoreType.REGULAR
        f32, bf16 = jnp.float32, jnp.bfloat16
        return pl.pallas_call(
            functools.partial(_kernel, consts),
            name="svgd",
            out_shape=pltpu.VMEM(particles.shape, f32),
            in_specs=[hbm, hbm, hbm, hbm],
            out_specs=vmem,
            scratch_shapes=[
                pltpu.VMEM((num_part, 2 * feat), f32),
                pltpu.VMEM((num_part, 2 * feat), f32),
                pltpu.VMEM((num_part, feat), f32),
                pltpu.VMEM((2, feat), f32),
                pltpu.VMEM((2, feat), f32),
                pltpu.VMEM((1, feat), f32),
                pltpu.VMEM((1, feat), f32),
                pltpu.VMEM((rank, feat), bf16),
                pltpu.VMEM((rank, feat), bf16),
                pltpu.VMEM((CHIPS, 6, HALF), f32),
                pltpu.VMEM((CHIPS, 6, HALF), f32),
                pltpu.VMEM((6, HALF), f32),
                pltpu.VMEM((2, CHIPS, 6, HALF), f32),
                pltpu.VMEM((1, HALF), f32),
                pltpu.VMEM((CHIPS, 1, HALF), f32),
                pltpu.VMEM((1, HALF), f32),
                pltpu.VMEM((2, 1, HALF), f32),
                pltpu.VMEM((HALF, 2 * feat), bf16),
                pltpu.VMEM((HALF, 2 * feat), bf16),
                dma((5,)), dma((4,)), dma((4,)), regular, regular, dma, dma, dma, dma((2,)), dma, dma, dma, dma((2,)), dma, dma, dma,
            ],
            compiler_params=pltpu.CompilerParams(collective_id=0, has_side_effects=True),
        )(particles, target_mean, precision.reshape(1, feat), low_factor.T)

    return jax.shard_map(local_steps, mesh=mesh, in_specs=(data_spec, mean_spec, prec_spec, factor_spec), out_specs=data_spec, check_vma=False)
```

time: 49.5 us -> 47.9 us (0.968)
  Pallas kernels: 48.6 us -> 47 us
    pallas_call x1, Pallas kernels: 48.6 us -> 47 us  [local_steps(): pl.pallas_call(functools.partial(_kernel, consts), name='svgd', out_shape...]
where the time goes in v5:
time: 47.9 us; the launch traced here: 47.8 us
  Pallas kernels  47 us (98%)
  local copies, waits for them, and re-layouts  0.8 us (2%)
    pallas_call x1, Pallas kernels, local_steps(): pl.pallas_call(functools.partial(_kernel, consts), name='svgd', out_shape...  47 us

profile of v5, /device:TPU:1, one launch (start us, length us, event | category | flops | bytes accessed | tf_op | source)
XLA Modules:
  0.0 47.8 jit_solution(9099222966696497309)
XLA Ops:
  0.0 47.0 %svgd.1 = f32[2,256,256]{2,1,0:T(8,128)S(1)} custom-call(f32[2,256,256]{2,1,0:T(8,128)} %part_ref.1, f32[2,256]{1,0:T(2,128)} %mean_ref.1, f32[1,256]{1,0:T(1,128)} %bitcast.3, bf16[64,256]{1,0:T(8,128)(2,1)} %bitcast.2), custom_call_target="tpu_custom_call" | custom-call | tf_op jit(solution)/shard_map/svgd/pallas_call | solution.py:295
  47.0 0.8 %copy.6 = f32[2,256,256]{2,1,0:T(8,128)} copy(f32[2,256,256]{2,1,0:T(8,128)S(1)} %svgd.1) | data formatting | bytes 1048576

commit v6 on v5

--- a/solution.py
+++ b/solution.py
@@ -13,6 +13,7 @@
 HALF = 128
 DIAG_CHIP = 21
 EARLY = (0,)
+LAG = 600
 MESH = pl.DeviceIdType.MESH
 NT = (((1,), (1,)), ((), ()))
 
@@ -29,6 +30,7 @@
             load_sem, swap_send, swap_recv, hello, go, rs_ssem, rs_rsem, ag_ssem, ag_rsem, dr_ssem, dr_rsem, dg_ssem, dg_rsem, ax_ssem, back_send, back_recv):
     two_over_h, inv_h, scale = consts
     rank, feat = factor_ref.shape
+    num_part = part_ref.shape[1]
     f32, bf16 = jnp.float32, jnp.bfloat16
     ens = lax.axis_index("ens")
     me = lax.axis_index("feat")
@@ -195,12 +197,14 @@
         keep = 1.0 + (scale * two_over_h) * jnp.sum(kernel, axis=1, keepdims=True)
         return kernel.astype(bf16), keep, proj
 
-    def moved(kernel_bf, keep, proj, th, still, cols):
+    def mixed(proj, still, cols):
         low = jnp.concatenate([
             jnp.dot(proj, u_lo[:, cols], preferred_element_type=f32),
             jnp.dot(proj, u_hi[:, cols], preferred_element_type=f32)], axis=0)
-        drive = jnp.dot(kernel_bf, (still - low).astype(bf16), preferred_element_type=f32)
-        return keep * th + scale * drive
+        return (still - low).astype(bf16)
+
+    def moved(kernel_bf, keep, proj, th, still, cols):
+        return keep * th + scale * jnp.dot(kernel_bf, mixed(proj, still, cols), preferred_element_type=f32)
 
     own = slice(0, feat)
     early = functools.reduce(jnp.logical_or, [chip == target for target in EARLY])
@@ -216,6 +220,10 @@
     @pl.when(core == 0)
     def _():
         pl.semaphore_wait(go, 1)
+
+    @pl.when(core == 0)
+    def _():
+        pl.delay(LAG)
 
     @pl.loop(0, NUM_STEPS - 1)
     def _(_):
@@ -268,8 +276,13 @@
     @pl.when(jnp.logical_not(early))
     def _():
         weights = kernel_matrix(0)
-        spare[...] = moved(*weights, theta[:, feat:], base[:, feat:], slice(feat, 2 * feat))
-        back_copy(spare, out_ref.at[core]).start()
+        kernel_bf, keep, proj = weights
+        partners = mixed(proj, base[:, feat:], slice(feat, 2 * feat))
+        step = num_part // 2
+        for r in range(0, num_part, step):
+            rows = slice(r, r + step)
+            spare[rows] = keep[rows] * theta[rows, feat:] + scale * jnp.dot(kernel_bf[rows], partners, preferred_element_type=f32)
+            back_copy(spare.at[pl.ds(r, step)], out_ref.at[core, pl.ds(r, step)]).start()
         out_ref[core] = moved(*weights, theta[:, own], base[:, own], own)
         back_copy(spare, out_ref.at[other]).wait()
 

time: 47.9 us -> 47.5 us (level)
  Pallas kernels: 47 us -> 46.4 us
    pallas_call x1, Pallas kernels: 47 us -> 46.4 us  [local_steps(): pl.pallas_call(functools.partial(_kernel, consts), name='svgd', out_shape...]
where the time goes in v6:
time: 47.5 us; the launch traced here: 47.2 us
  Pallas kernels  46.4 us (98%)
  local copies, waits for them, and re-layouts  0.8 us (2%)
    pallas_call x1, Pallas kernels, local_steps(): pl.pallas_call(functools.partial(_kernel, consts), name='svgd', out_shape...  46.4 us

profile of v6, /device:TPU:1, one launch (start us, length us, event | category | flops | bytes accessed | tf_op | source)
XLA Modules:
  0.0 47.2 jit_solution(12854528595745475547)
XLA Ops:
  0.0 46.4 %svgd.1 = f32[2,256,256]{2,1,0:T(8,128)S(1)} custom-call(f32[2,256,256]{2,1,0:T(8,128)} %part_ref.1, f32[2,256]{1,0:T(2,128)} %mean_ref.1, f32[1,256]{1,0:T(1,128)} %bitcast.3, bf16[64,256]{1,0:T(8,128)(2,1)} %bitcast.2), custom_call_target="tpu_custom_call" | custom-call | tf_op jit(solution)/shard_map/svgd/pallas_call | solution.py:308
  46.4 0.8 %copy.6 = f32[2,256,256]{2,1,0:T(8,128)} copy(f32[2,256,256]{2,1,0:T(8,128)S(1)} %svgd.1) | data formatting | bytes 1048576

commit v7 on v6

--- a/solution.py
+++ b/solution.py
@@ -225,9 +225,10 @@
     def _():
         pl.delay(LAG)
 
+    scatter()
+
     @pl.loop(0, NUM_STEPS - 1)
     def _(_):
-        scatter()
         base[...] = -((theta[...] - mean_row) * prec_row) - two_over_h * theta[...]
         reduce()
         all_gather(False)
@@ -238,12 +239,11 @@
             cols = slice(part * feat, (part + 1) * feat)
             theta[:, cols] = moved(*weights, theta[:, cols], base[:, cols], cols)
         partials()
+        scatter()
         sent(False)
 
     def still(th, mean, prec):
         return -((th - mean) * prec) - two_over_h * th
-
-    scatter()
 
     def back_copy(src, dst):
         return pltpu.make_async_remote_copy(src, dst, back_send, back_recv, device_id=(ens, partner), device_id_type=MESH)

time: 47.5 us -> 47.4 us (level)
  no operation moved by 1% of the time
where the time goes in v7:
time: 47.4 us; the launch traced here: 47.2 us
  Pallas kernels  46.4 us (98%)
  local copies, waits for them, and re-layouts  0.8 us (2%)
    pallas_call x1, Pallas kernels, local_steps(): pl.pallas_call(functools.partial(_kernel, consts), name='svgd', out_shape...  46.4 us

profile of v7, /device:TPU:1, one launch (start us, length us, event | category | flops | bytes accessed | tf_op | source)
XLA Modules:
  0.0 47.2 jit_solution(17908449535717975548)
XLA Ops:
  0.0 46.4 %svgd.1 = f32[2,256,256]{2,1,0:T(8,128)S(1)} custom-call(f32[2,256,256]{2,1,0:T(8,128)} %part_ref.1, f32[2,256]{1,0:T(2,128)} %mean_ref.1, f32[1,256]{1,0:T(1,128)} %bitcast.3, bf16[64,256]{1,0:T(8,128)(2,1)} %bitcast.2), custom_call_target="tpu_custom_call" | custom-call | tf_op jit(solution)/shard_map/svgd/pallas_call | solution.py:308
  46.4 0.8 %copy.6 = f32[2,256,256]{2,1,0:T(8,128)} copy(f32[2,256,256]{2,1,0:T(8,128)S(1)} %svgd.1) | data formatting | bytes 1048576

commit v8 on v7

--- a/solution.py
+++ b/solution.py
@@ -26,7 +26,7 @@
 
 
 def _kernel(consts, part_ref, mean_ref, prec_ref, factor_ref, out_ref,
-            theta, base, spare, mean_own, mean_x, prec_own, prec_x, factor_own, factor_x, rs_send, rs_recv, total, gather, diag_send, diag_recv, diag_total, diag_all, u_lo, u_hi,
+            theta, base, spare, mean_own, mean_x, prec_own, prec_x, factor_own, factor_x, rs_send, rs_recv, total, gather, diag_send, diag_recv, diag_total, diag_all, u_two,
             load_sem, swap_send, swap_recv, hello, go, rs_ssem, rs_rsem, ag_ssem, ag_rsem, dr_ssem, dr_rsem, dg_ssem, dg_rsem, ax_ssem, back_send, back_recv):
     two_over_h, inv_h, scale = consts
     rank, feat = factor_ref.shape
@@ -84,14 +84,11 @@
     col_id = lax.broadcasted_iota(jnp.int32, (HALF, HALF), 1)
     eye, upper = row_id == col_id, row_id <= col_id
 
-    zeros = jnp.zeros((HALF - rank, 2 * feat), bf16)
-    u_lo[rank:, :] = zeros
-    u_hi[:HALF - rank, :] = zeros
     for copy in swaps:
         copy.wait_recv()
     factor = jnp.concatenate([factor_own[...], factor_x[...]], axis=1)
-    u_lo[:rank, :] = factor
-    u_hi[HALF - rank:, :] = factor
+    u_two[:rank, :] = factor
+    u_two[rank:, :] = factor
     mean_row = jnp.concatenate([mean_own[pl.ds(core, 1), :], mean_x[pl.ds(core, 1), :]], axis=1)
     prec_row = jnp.concatenate([prec_own[...], prec_x[...]], axis=1)
     others = pl.ds(0, CHIPS - 1)
@@ -103,12 +100,11 @@
         th = theta[...]
         tb = th.astype(bf16)
         xb = (th - mean_row).astype(bf16)
-        top = lax.dot_general(tb[:HALF], tb, NT, preferred_element_type=f32)
-        low = lax.dot_general(tb[HALF:], tb[HALF:], NT, preferred_element_type=f32)
-        proj = (lax.dot_general(xb[:HALF], u_lo[...], NT, preferred_element_type=f32)
-                + lax.dot_general(xb[HALF:], u_hi[...], NT, preferred_element_type=f32))
-        tri = jnp.where(upper, top[:, :HALF], low)
-        cross = top[:, HALF:]
+        gram = lax.dot_general(tb, tb, NT, preferred_element_type=f32)
+        twice = lax.dot_general(xb, u_two[...], NT, preferred_element_type=f32)
+        proj = jnp.where(col_id < rank, twice[:HALF], twice[HALF:])
+        cross, low = gram[:HALF, HALF:], gram[HALF:, HALF:]
+        tri = jnp.where(upper, gram[:HALF, :HALF], low)
         diag = jnp.sum(jnp.where(eye, low, 0.0), axis=0, keepdims=True)
         for o in range(CHIPS):
             block, r = (cross, 4 * o) if o < CHIPS // 2 else (tri, 4 * o - HALF)
@@ -181,7 +177,8 @@
         diag = diag_all[k]
         cross = jnp.concatenate([gather[k, o, 0:4, :] for o in range(CHIPS // 2)], axis=0)
         tri = jnp.concatenate([gather[k, o, 0:4, :] for o in range(CHIPS // 2, CHIPS)], axis=0)
-        proj = jnp.concatenate([gather[k, o, 4:6, :] for o in range(CHIPS)], axis=0).astype(bf16)
+        proj = jnp.concatenate([gather[k, o, 4:6, :] for o in range(CHIPS)], axis=0)
+        proj = jnp.concatenate([jnp.where(col_id < rank, proj, 0.0), jnp.where(col_id < rank, 0.0, proj)], axis=0).astype(bf16)
         tri_t, cross_t = tri.T, cross.T
         g_aa = jnp.where(upper, tri, tri_t)
         g_cc = jnp.where(eye, diag, jnp.where(upper, tri_t, tri))
@@ -198,10 +195,7 @@
         return kernel.astype(bf16), keep, proj
 
     def mixed(proj, still, cols):
-        low = jnp.concatenate([
-            jnp.dot(proj, u_lo[:, cols], preferred_element_type=f32),
-            jnp.dot(proj, u_hi[:, cols], preferred_element_type=f32)], axis=0)
-        return (still - low).astype(bf16)
+        return (still - jnp.dot(proj, u_two[:, cols], preferred_element_type=f32)).astype(bf16)
 
     def moved(kernel_bf, keep, proj, th, still, cols):
         return keep * th + scale * jnp.dot(kernel_bf, mixed(proj, still, cols), preferred_element_type=f32)
@@ -235,9 +229,7 @@
         drain(diag_all.at[0], dg_rsem.at[0])
         drain(gather.at[0], ag_rsem.at[0])
         weights = kernel_matrix(0)
-        for part in range(2):
-            cols = slice(part * feat, (part + 1) * feat)
-            theta[:, cols] = moved(*weights, theta[:, cols], base[:, cols], cols)
+        theta[...] = moved(*weights, theta[...], base[...], slice(0, 2 * feat))
         partials()
         scatter()
         sent(False)
@@ -329,8 +321,7 @@
                 pltpu.VMEM((CHIPS, 1, HALF), f32),
                 pltpu.VMEM((1, HALF), f32),
                 pltpu.VMEM((2, 1, HALF), f32),
-                pltpu.VMEM((HALF, 2 * feat), bf16),
-                pltpu.VMEM((HALF, 2 * feat), bf16),
+                pltpu.VMEM((2 * rank, 2 * feat), bf16),
                 dma((5,)), dma((4,)), dma((4,)), regular, regular, dma, dma, dma, dma((2,)), dma, dma, dma, dma((2,)), dma, dma, dma,
             ],
             compiler_params=pltpu.CompilerParams(collective_id=0, has_side_effects=True),

time: 47.4 us -> 46.9 us (0.989)
  Pallas kernels: 46.4 us -> 45.9 us
    pallas_call x1, Pallas kernels: 46.4 us -> 45.9 us  [local_steps(): pl.pallas_call(functools.partial(_kernel, consts), name='svgd', out_shape...]
where the time goes in v8:
time: 46.9 us; the launch traced here: 46.7 us
  Pallas kernels  45.9 us (98%)
  local copies, waits for them, and re-layouts  0.8 us (2%)
    pallas_call x1, Pallas kernels, local_steps(): pl.pallas_call(functools.partial(_kernel, consts), name='svgd', out_shape...  45.9 us

profile of v8, /device:TPU:1, one launch (start us, length us, event | category | flops | bytes accessed | tf_op | source)
XLA Modules:
  0.0 46.7 jit_solution(4063490745076531943)
XLA Ops:
  0.0 45.9 %svgd.1 = f32[2,256,256]{2,1,0:T(8,128)S(1)} custom-call(f32[2,256,256]{2,1,0:T(8,128)} %part_ref.1, f32[2,256]{1,0:T(2,128)} %mean_ref.1, f32[1,256]{1,0:T(1,128)} %bitcast.3, bf16[64,256]{1,0:T(8,128)(2,1)} %bitcast.2), custom_call_target="tpu_custom_call" | custom-call | tf_op jit(solution)/shard_map/svgd/pallas_call | solution.py:300
  45.9 0.8 %copy.6 = f32[2,256,256]{2,1,0:T(8,128)} copy(f32[2,256,256]{2,1,0:T(8,128)S(1)} %svgd.1) | data formatting | bytes 1048576

commit v9 on v8

--- a/solution.py
+++ b/solution.py
@@ -11,7 +11,7 @@
 SIDE = 4
 CHIPS = SIDE ** 3
 HALF = 128
-DIAG_CHIP = 21
+DIAG_CHIP = 20
 EARLY = (0,)
 LAG = 600
 MESH = pl.DeviceIdType.MESH
@@ -96,8 +96,7 @@
     def drain(ref, sem):
         pltpu.make_async_copy(ref, ref, sem).wait()
 
-    def partials():
-        th = theta[...]
+    def partials(th):
         tb = th.astype(bf16)
         xb = (th - mean_row).astype(bf16)
         gram = lax.dot_general(tb, tb, NT, preferred_element_type=f32)
@@ -202,7 +201,7 @@
 
     own = slice(0, feat)
     early = functools.reduce(jnp.logical_or, [chip == target for target in EARLY])
-    partials()
+    partials(theta[...])
     for copy in swaps:
         copy.wait_send()
 
@@ -229,8 +228,9 @@
         drain(diag_all.at[0], dg_rsem.at[0])
         drain(gather.at[0], ag_rsem.at[0])
         weights = kernel_matrix(0)
-        theta[...] = moved(*weights, theta[...], base[...], slice(0, 2 * feat))
-        partials()
+        new = moved(*weights, theta[...], base[...], slice(0, 2 * feat))
+        theta[...] = new
+        partials(new)
         scatter()
         sent(False)
 

time: 46.9 us -> 46.9 us (level)
  no operation moved by 1% of the time
where the time goes in v9:
time: 46.9 us; the launch traced here: 46.7 us
  Pallas kernels  45.9 us (98%)
  local copies, waits for them, and re-layouts  0.8 us (2%)
    pallas_call x1, Pallas kernels, local_steps(): pl.pallas_call(functools.partial(_kernel, consts), name='svgd', out_shape...  45.9 us

profile of v9, /device:TPU:1, one launch (start us, length us, event | category | flops | bytes accessed | tf_op | source)
XLA Modules:
  0.0 46.7 jit_solution(11762589332891496567)
XLA Ops:
  0.0 45.9 %svgd.1 = f32[2,256,256]{2,1,0:T(8,128)S(1)} custom-call(f32[2,256,256]{2,1,0:T(8,128)} %part_ref.1, f32[2,256]{1,0:T(2,128)} %mean_ref.1, f32[1,256]{1,0:T(1,128)} %bitcast.3, bf16[64,256]{1,0:T(8,128)(2,1)} %bitcast.2), custom_call_target="tpu_custom_call" | custom-call | tf_op jit(solution)/shard_map/svgd/pallas_call | solution.py:300
  45.9 0.8 %copy.6 = f32[2,256,256]{2,1,0:T(8,128)} copy(f32[2,256,256]{2,1,0:T(8,128)S(1)} %svgd.1) | data formatting | bytes 1048576

commit v10 on v9

--- a/solution.py
+++ b/solution.py
@@ -124,10 +124,10 @@
 
     def reduce():
         drain(rs_recv, rs_rsem)
-        sums = [rs_recv[o] for o in range(4)]
-        for o in range(4, CHIPS):
-            sums[o % 4] = sums[o % 4] + rs_recv[o]
-        total[...] = (sums[0] + sums[1]) + (sums[2] + sums[3])
+        terms = [rs_recv[o] for o in range(CHIPS)]
+        while len(terms) > 1:
+            terms = [a + b for a, b in zip(terms[::2], terms[1::2])]
+        total[...] = terms[0]
 
     def reduce_diag():
         drain(diag_recv, dr_rsem)
@@ -270,7 +270,7 @@
         weights = kernel_matrix(0)
         kernel_bf, keep, proj = weights
         partners = mixed(proj, base[:, feat:], slice(feat, 2 * feat))
-        step = num_part // 2
+        step = num_part // 4
         for r in range(0, num_part, step):
             rows = slice(r, r + step)
             spare[rows] = keep[rows] * theta[rows, feat:] + scale * jnp.dot(kernel_bf[rows], partners, preferred_element_type=f32)

time: 46.9 us -> 46.8 us (level)
  no operation moved by 1% of the time
where the time goes in v10:
time: 46.8 us; the launch traced here: 46.7 us
  Pallas kernels  45.9 us (98%)
  local copies, waits for them, and re-layouts  0.8 us (2%)
    pallas_call x1, Pallas kernels, local_steps(): pl.pallas_call(functools.partial(_kernel, consts), name='svgd', out_shape...  45.9 us

profile of v10, /device:TPU:1, one launch (start us, length us, event | category | flops | bytes accessed | tf_op | source)
XLA Modules:
  0.0 46.7 jit_solution(13674022670564703678)
XLA Ops:
  0.0 45.9 %svgd.1 = f32[2,256,256]{2,1,0:T(8,128)S(1)} custom-call(f32[2,256,256]{2,1,0:T(8,128)} %part_ref.1, f32[2,256]{1,0:T(2,128)} %mean_ref.1, f32[1,256]{1,0:T(1,128)} %bitcast.3, bf16[64,256]{1,0:T(8,128)(2,1)} %bitcast.2), custom_call_target="tpu_custom_call" | custom-call | tf_op jit(solution)/shard_map/svgd/pallas_call | solution.py:300
  45.9 0.8 %copy.6 = f32[2,256,256]{2,1,0:T(8,128)} copy(f32[2,256,256]{2,1,0:T(8,128)S(1)} %svgd.1) | data formatting | bytes 1048576
